TPU v7x, 32 devices: a 4x2x2 block of a 4x4x8 slice. The times are simulated.
32 devices in a mesh: rep: 4 (over y, z), shard: 8 (over x, core).
Axes of the slice: x: 4, y: 2, z: 2, core: 2. Of those that a mesh axis runs over, the one named last changes fastest.
The devices are a block of a 4x4x8 slice.
Arguments:
- ratings: float32 [4096, 4096], P(('rep', 'shard')), parts along dimension 0
- observed: int32 [4096, 4096], P(('rep', 'shard')), parts along dimension 0
- user_init: float32 [4096, 32], P(('rep', 'shard')), parts along dimension 0
- item_init: float32 [16384, 32], P(('rep', 'shard')), parts along dimension 0
Outputs:
- output 1: float32 [4096, 32], P(('rep', 'shard')), parts along dimension 0
- output 2: float32 [16384, 32], P(('rep', 'shard')), parts along dimension 0
There are 4 independent parts. A program takes and returns all parts, laid end to end along the dimension named above; each array names one.
All inputs are finite; a program needn't handle non-finite values.
Results may differ from a plain program's by a relative error of at most 0.001.
Values are sent between devices in bfloat16 or wider.
A program may use at most 768 MiB of HBM per device.

v0:
```python
import jax
import jax.numpy as jnp
import math
from jax import lax
from jax.sharding import PartitionSpec as P

STRATUM_STEPS = 4
EPOCHS = 2


def solution(mesh):
    group_devs = mesh.shape["shard"]
    row_spec = P(("rep", "shard"), None)
    shift_back = [(source, (source - 1) % group_devs) for source in range(group_devs)]

    def local(ratings, observed, user_init, item_init):
        users_dev = ratings.shape[0]
        items_dev, factor_rank = item_init.shape
        step_scale = (users_dev + items_dev + factor_rank) / math.sqrt(factor_rank)
        step_size = 0.5 / step_scale
        weight_decay = 0.03 * math.sqrt(users_dev * items_dev / factor_rank)
        seen_all = observed != 0
        my_index = lax.axis_index("shard")

        def stratum(stratum_idx, state_pair):
            user_blk, item_blk = state_pair
            col_start = ((my_index + stratum_idx) % group_devs) * items_dev
            rating_blk = lax.dynamic_slice_in_dim(ratings, col_start, items_dev, axis=1)
            seen_blk = lax.dynamic_slice_in_dim(seen_all, col_start, items_dev, axis=1)

            def step(unused, inner_pair):
                user_cur, item_cur = inner_pair
                item_bf = item_cur.astype(jnp.bfloat16)
                predicted = jnp.einsum("ur,ir->ui", user_cur.astype(jnp.bfloat16), item_bf, preferred_element_type=jnp.float32)
                residual = jnp.where(seen_blk, predicted - rating_blk, 0.0).astype(jnp.bfloat16)
                grad_user = jnp.dot(residual, item_bf, preferred_element_type=jnp.float32)
                user_new = user_cur - step_size * (grad_user + weight_decay * user_cur)
                user_bf = user_new.astype(jnp.bfloat16)
                predicted = jnp.einsum("ur,ir->ui", user_bf, item_bf, preferred_element_type=jnp.float32)
                residual = jnp.where(seen_blk, predicted - rating_blk, 0.0).astype(jnp.bfloat16)
                grad_item = jnp.einsum("ui,ur->ir", residual, user_bf, preferred_element_type=jnp.float32)
                item_new = item_cur - step_size * (grad_item + weight_decay * item_cur)
                return user_new, item_new

            user_blk, item_blk = lax.fori_loop(0, STRATUM_STEPS, step, (user_blk, item_blk))
            item_blk = lax.ppermute(item_blk, "shard", shift_back)
            return user_blk, item_blk

        return lax.fori_loop(0, EPOCHS * group_devs, stratum, (user_init, item_init))

    return jax.shard_map(local, mesh=mesh, in_specs=(row_spec, row_spec, row_spec, row_spec), out_specs=(row_spec, row_spec), check_vma=False)
```

profile of v0, /device:TPU:95, one launch (start us, length us, event | category | flops | bytes accessed | tf_op | source)
XLA Modules:
  0.0 144.2 jit_solution(13767346103957014770)
XLA Ops:
  0.7 1.9 %broadcast_compare_fusion = pred[128,4096]{1,0:T(32,128)(4,1)S(1)} fusion(s32[128,4096]{1,0:T(8,128)} %param.9), kind=kLoop, calls=%fused_computation.24 | loop fusion | flops 524288 | bytes 2621440 | tf_op jit(solution)/shard_map/ne | solution.py:22
  2.6 141.0 %while.53 = (s32[]{:T(128)}, f32[128,32]{0,1:T(8,128)S(1)}, f32[512,32]{0,1:T(8,128)S(1)}, s32[]{:T(128)}, f32[128,4096]{1,0:T(8,128)}, /*index=5*/pred[128,4096...) while((s32[]{:T(128)}, f32[128,32]{0,1:T(8,128)S(1)}, ...), condition=%wide.region_3.4_spmd, body=%wide.region_0.3_spmd.sunk | while | flops 17313808 | bytes 2114001 | solution.py:49
  2.6 1.0 constant_dynamic-slice_fusion.4
  3.6 2.9 %while.54 = (s32[]{:T(128)}, f32[128,32]{0,1:T(8,128)S(1)}, f32[512,32]{0,1:T(8,128)S(1)}, f32[128,512]{1,0:T(8,128)S(1)}, pred[128,512]{1,0:T(32,128)(4,1)S(1)}, /*index=5*/s32[]{:T(128)}) while((s32[]{:T(128)}, f32[128,32]{0,1:T(8,128)S(1)}, f32[512,32]{0,1:T(8,128)S(1)}, f32[128,512]{1,0:T(8,128)S(1)}, pred[128,512]{1,0:T(32,128)(4,1)S(1)}, ...), condition=%wide.region_2.2_spmd, body=%wide.region_1.1_spmd.sunk | while | flops 17313792 | bytes 1065029 | solution.py:45
  7.1 4.3 %collective-permute-done = f32[512,32]{0,1:T(8,128)S(1)} collective-permute-done((f32[512,32]{0,1:T(8,128)S(1)}, f32[512,32]{0,1:T(8,128)S(1)}, u32[]{:S(2)}, u32[]{:S(2)}) %collective-permute-start) | collective-permute-done | bytes 65568 | tf_op jit(solution)/shard_map/while/body/eval_jaxpr/ppermute | solution.py:46
  11.4 1.0 constant_dynamic-slice_fusion.4
  12.4 2.9 %while.54 = (s32[]{:T(128)}, f32[128,32]{0,1:T(8,128)S(1)}, f32[512,32]{0,1:T(8,128)S(1)}, f32[128,512]{1,0:T(8,128)S(1)}, pred[128,512]{1,0:T(32,128)(4,1)S(1)}, /*index=5*/s32[]{:T(128)}) while((s32[]{:T(128)}, f32[128,32]{0,1:T(8,128)S(1)}, f32[512,32]{0,1:T(8,128)S(1)}, f32[128,512]{1,0:T(8,128)S(1)}, pred[128,512]{1,0:T(32,128)(4,1)S(1)}, ...), condition=%wide.region_2.2_spmd, body=%wide.region_1.1_spmd.sunk | while | flops 17313792 | bytes 1065029 | solution.py:45
  15.4 4.9 %collective-permute-done = f32[512,32]{0,1:T(8,128)S(1)} collective-permute-done((f32[512,32]{0,1:T(8,128)S(1)}, f32[512,32]{0,1:T(8,128)S(1)}, u32[]{:S(2)}, u32[]{:S(2)}) %collective-permute-start) | collective-permute-done | bytes 65568 | tf_op jit(solution)/shard_map/while/body/eval_jaxpr/ppermute | solution.py:46
  20.3 1.0 constant_dynamic-slice_fusion.4
  21.2 2.9 %while.54 = (s32[]{:T(128)}, f32[128,32]{0,1:T(8,128)S(1)}, f32[512,32]{0,1:T(8,128)S(1)}, f32[128,512]{1,0:T(8,128)S(1)}, pred[128,512]{1,0:T(32,128)(4,1)S(1)}, /*index=5*/s32[]{:T(128)}) while((s32[]{:T(128)}, f32[128,32]{0,1:T(8,128)S(1)}, f32[512,32]{0,1:T(8,128)S(1)}, f32[128,512]{1,0:T(8,128)S(1)}, pred[128,512]{1,0:T(32,128)(4,1)S(1)}, ...), condition=%wide.region_2.2_spmd, body=%wide.region_1.1_spmd.sunk | while | flops 17313792 | bytes 1065029 | solution.py:45
  24.2 4.9 %collective-permute-done = f32[512,32]{0,1:T(8,128)S(1)} collective-permute-done((f32[512,32]{0,1:T(8,128)S(1)}, f32[512,32]{0,1:T(8,128)S(1)}, u32[]{:S(2)}, u32[]{:S(2)}) %collective-permute-start) | collective-permute-done | bytes 65568 | tf_op jit(solution)/shard_map/while/body/eval_jaxpr/ppermute | solution.py:46
  29.1 1.0 constant_dynamic-slice_fusion.4
  30.0 2.9 %while.54 = (s32[]{:T(128)}, f32[128,32]{0,1:T(8,128)S(1)}, f32[512,32]{0,1:T(8,128)S(1)}, f32[128,512]{1,0:T(8,128)S(1)}, pred[128,512]{1,0:T(32,128)(4,1)S(1)}, /*index=5*/s32[]{:T(128)}) while((s32[]{:T(128)}, f32[128,32]{0,1:T(8,128)S(1)}, f32[512,32]{0,1:T(8,128)S(1)}, f32[128,512]{1,0:T(8,128)S(1)}, pred[128,512]{1,0:T(32,128)(4,1)S(1)}, ...), condition=%wide.region_2.2_spmd, body=%wide.region_1.1_spmd.sunk | while | flops 17313792 | bytes 1065029 | solution.py:45
  33.0 4.9 %collective-permute-done = f32[512,32]{0,1:T(8,128)S(1)} collective-permute-done((f32[512,32]{0,1:T(8,128)S(1)}, f32[512,32]{0,1:T(8,128)S(1)}, u32[]{:S(2)}, u32[]{:S(2)}) %collective-permute-start) | collective-permute-done | bytes 65568 | tf_op jit(solution)/shard_map/while/body/eval_jaxpr/ppermute | solution.py:46
  37.9 1.0 constant_dynamic-slice_fusion.4
  38.8 2.9 %while.54 = (s32[]{:T(128)}, f32[128,32]{0,1:T(8,128)S(1)}, f32[512,32]{0,1:T(8,128)S(1)}, f32[128,512]{1,0:T(8,128)S(1)}, pred[128,512]{1,0:T(32,128)(4,1)S(1)}, /*index=5*/s32[]{:T(128)}) while((s32[]{:T(128)}, f32[128,32]{0,1:T(8,128)S(1)}, f32[512,32]{0,1:T(8,128)S(1)}, f32[128,512]{1,0:T(8,128)S(1)}, pred[128,512]{1,0:T(32,128)(4,1)S(1)}, ...), condition=%wide.region_2.2_spmd, body=%wide.region_1.1_spmd.sunk | while | flops 17313792 | bytes 1065029 | solution.py:45
  41.8 4.9 %collective-permute-done = f32[512,32]{0,1:T(8,128)S(1)} collective-permute-done((f32[512,32]{0,1:T(8,128)S(1)}, f32[512,32]{0,1:T(8,128)S(1)}, u32[]{:S(2)}, u32[]{:S(2)}) %collective-permute-start) | collective-permute-done | bytes 65568 | tf_op jit(solution)/shard_map/while/body/eval_jaxpr/ppermute | solution.py:46
  46.7 1.0 constant_dynamic-slice_fusion.4
  47.7 2.9 %while.54 = (s32[]{:T(128)}, f32[128,32]{0,1:T(8,128)S(1)}, f32[512,32]{0,1:T(8,128)S(1)}, f32[128,512]{1,0:T(8,128)S(1)}, pred[128,512]{1,0:T(32,128)(4,1)S(1)}, /*index=5*/s32[]{:T(128)}) while((s32[]{:T(128)}, f32[128,32]{0,1:T(8,128)S(1)}, f32[512,32]{0,1:T(8,128)S(1)}, f32[128,512]{1,0:T(8,128)S(1)}, pred[128,512]{1,0:T(32,128)(4,1)S(1)}, ...), condition=%wide.region_2.2_spmd, body=%wide.region_1.1_spmd.sunk | while | flops 17313792 | bytes 1065029 | solution.py:45
  50.6 4.9 %collective-permute-done = f32[512,32]{0,1:T(8,128)S(1)} collective-permute-done((f32[512,32]{0,1:T(8,128)S(1)}, f32[512,32]{0,1:T(8,128)S(1)}, u32[]{:S(2)}, u32[]{:S(2)}) %collective-permute-start) | collective-permute-done | bytes 65568 | tf_op jit(solution)/shard_map/while/body/eval_jaxpr/ppermute | solution.py:46
  55.5 1.0 constant_dynamic-slice_fusion.4
  56.5 2.9 %while.54 = (s32[]{:T(128)}, f32[128,32]{0,1:T(8,128)S(1)}, f32[512,32]{0,1:T(8,128)S(1)}, f32[128,512]{1,0:T(8,128)S(1)}, pred[128,512]{1,0:T(32,128)(4,1)S(1)}, /*index=5*/s32[]{:T(128)}) while((s32[]{:T(128)}, f32[128,32]{0,1:T(8,128)S(1)}, f32[512,32]{0,1:T(8,128)S(1)}, f32[128,512]{1,0:T(8,128)S(1)}, pred[128,512]{1,0:T(32,128)(4,1)S(1)}, ...), condition=%wide.region_2.2_spmd, body=%wide.region_1.1_spmd.sunk | while | flops 17313792 | bytes 1065029 | solution.py:45
  59.4 4.9 %collective-permute-done = f32[512,32]{0,1:T(8,128)S(1)} collective-permute-done((f32[512,32]{0,1:T(8,128)S(1)}, f32[512,32]{0,1:T(8,128)S(1)}, u32[]{:S(2)}, u32[]{:S(2)}) %collective-permute-start) | collective-permute-done | bytes 65568 | tf_op jit(solution)/shard_map/while/body/eval_jaxpr/ppermute | solution.py:46
  64.3 1.0 constant_dynamic-slice_fusion.4
  65.3 2.9 %while.54 = (s32[]{:T(128)}, f32[128,32]{0,1:T(8,128)S(1)}, f32[512,32]{0,1:T(8,128)S(1)}, f32[128,512]{1,0:T(8,128)S(1)}, pred[128,512]{1,0:T(32,128)(4,1)S(1)}, /*index=5*/s32[]{:T(128)}) while((s32[]{:T(128)}, f32[128,32]{0,1:T(8,128)S(1)}, f32[512,32]{0,1:T(8,128)S(1)}, f32[128,512]{1,0:T(8,128)S(1)}, pred[128,512]{1,0:T(32,128)(4,1)S(1)}, ...), condition=%wide.region_2.2_spmd, body=%wide.region_1.1_spmd.sunk | while | flops 17313792 | bytes 1065029 | solution.py:45
  68.2 4.9 %collective-permute-done = f32[512,32]{0,1:T(8,128)S(1)} collective-permute-done((f32[512,32]{0,1:T(8,128)S(1)}, f32[512,32]{0,1:T(8,128)S(1)}, u32[]{:S(2)}, u32[]{:S(2)}) %collective-permute-start) | collective-permute-done | bytes 65568 | tf_op jit(solution)/shard_map/while/body/eval_jaxpr/ppermute | solution.py:46
  73.1 1.0 constant_dynamic-slice_fusion.4
  74.1 2.9 %while.54 = (s32[]{:T(128)}, f32[128,32]{0,1:T(8,128)S(1)}, f32[512,32]{0,1:T(8,128)S(1)}, f32[128,512]{1,0:T(8,128)S(1)}, pred[128,512]{1,0:T(32,128)(4,1)S(1)}, /*index=5*/s32[]{:T(128)}) while((s32[]{:T(128)}, f32[128,32]{0,1:T(8,128)S(1)}, f32[512,32]{0,1:T(8,128)S(1)}, f32[128,512]{1,0:T(8,128)S(1)}, pred[128,512]{1,0:T(32,128)(4,1)S(1)}, ...), condition=%wide.region_2.2_spmd, body=%wide.region_1.1_spmd.sunk | while | flops 17313792 | bytes 1065029 | solution.py:45
  77.0 4.9 %collective-permute-done = f32[512,32]{0,1:T(8,128)S(1)} collective-permute-done((f32[512,32]{0,1:T(8,128)S(1)}, f32[512,32]{0,1:T(8,128)S(1)}, u32[]{:S(2)}, u32[]{:S(2)}) %collective-permute-start) | collective-permute-done | bytes 65568 | tf_op jit(solution)/shard_map/while/body/eval_jaxpr/ppermute | solution.py:46
  81.9 1.0 constant_dynamic-slice_fusion.4
  82.9 2.9 %while.54 = (s32[]{:T(128)}, f32[128,32]{0,1:T(8,128)S(1)}, f32[512,32]{0,1:T(8,128)S(1)}, f32[128,512]{1,0:T(8,128)S(1)}, pred[128,512]{1,0:T(32,128)(4,1)S(1)}, /*index=5*/s32[]{:T(128)}) while((s32[]{:T(128)}, f32[128,32]{0,1:T(8,128)S(1)}, f32[512,32]{0,1:T(8,128)S(1)}, f32[128,512]{1,0:T(8,128)S(1)}, pred[128,512]{1,0:T(32,128)(4,1)S(1)}, ...), condition=%wide.region_2.2_spmd, body=%wide.region_1.1_spmd.sunk | while | flops 17313792 | bytes 1065029 | solution.py:45
  85.8 4.9 %collective-permute-done = f32[512,32]{0,1:T(8,128)S(1)} collective-permute-done((f32[512,32]{0,1:T(8,128)S(1)}, f32[512,32]{0,1:T(8,128)S(1)}, u32[]{:S(2)}, u32[]{:S(2)}) %collective-permute-start) | collective-permute-done | bytes 65568 | tf_op jit(solution)/shard_map/while/body/eval_jaxpr/ppermute | solution.py:46
  90.7 1.0 constant_dynamic-slice_fusion.4
  91.7 2.9 %while.54 = (s32[]{:T(128)}, f32[128,32]{0,1:T(8,128)S(1)}, f32[512,32]{0,1:T(8,128)S(1)}, f32[128,512]{1,0:T(8,128)S(1)}, pred[128,512]{1,0:T(32,128)(4,1)S(1)}, /*index=5*/s32[]{:T(128)}) while((s32[]{:T(128)}, f32[128,32]{0,1:T(8,128)S(1)}, f32[512,32]{0,1:T(8,128)S(1)}, f32[128,512]{1,0:T(8,128)S(1)}, pred[128,512]{1,0:T(32,128)(4,1)S(1)}, ...), condition=%wide.region_2.2_spmd, body=%wide.region_1.1_spmd.sunk | while | flops 17313792 | bytes 1065029 | solution.py:45
  94.6 4.9 %collective-permute-done = f32[512,32]{0,1:T(8,128)S(1)} collective-permute-done((f32[512,32]{0,1:T(8,128)S(1)}, f32[512,32]{0,1:T(8,128)S(1)}, u32[]{:S(2)}, u32[]{:S(2)}) %collective-permute-start) | collective-permute-done | bytes 65568 | tf_op jit(solution)/shard_map/while/body/eval_jaxpr/ppermute | solution.py:46
  99.5 1.0 constant_dynamic-slice_fusion.4
  100.5 2.9 %while.54 = (s32[]{:T(128)}, f32[128,32]{0,1:T(8,128)S(1)}, f32[512,32]{0,1:T(8,128)S(1)}, f32[128,512]{1,0:T(8,128)S(1)}, pred[128,512]{1,0:T(32,128)(4,1)S(1)}, /*index=5*/s32[]{:T(128)}) while((s32[]{:T(128)}, f32[128,32]{0,1:T(8,128)S(1)}, f32[512,32]{0,1:T(8,128)S(1)}, f32[128,512]{1,0:T(8,128)S(1)}, pred[128,512]{1,0:T(32,128)(4,1)S(1)}, ...), condition=%wide.region_2.2_spmd, body=%wide.region_1.1_spmd.sunk | while | flops 17313792 | bytes 1065029 | solution.py:45
  103.4 4.9 %collective-permute-done = f32[512,32]{0,1:T(8,128)S(1)} collective-permute-done((f32[512,32]{0,1:T(8,128)S(1)}, f32[512,32]{0,1:T(8,128)S(1)}, u32[]{:S(2)}, u32[]{:S(2)}) %collective-permute-start) | collective-permute-done | bytes 65568 | tf_op jit(solution)/shard_map/while/body/eval_jaxpr/ppermute | solution.py:46
  108.3 1.0 constant_dynamic-slice_fusion.4
  109.3 2.9 %while.54 = (s32[]{:T(128)}, f32[128,32]{0,1:T(8,128)S(1)}, f32[512,32]{0,1:T(8,128)S(1)}, f32[128,512]{1,0:T(8,128)S(1)}, pred[128,512]{1,0:T(32,128)(4,1)S(1)}, /*index=5*/s32[]{:T(128)}) while((s32[]{:T(128)}, f32[128,32]{0,1:T(8,128)S(1)}, f32[512,32]{0,1:T(8,128)S(1)}, f32[128,512]{1,0:T(8,128)S(1)}, pred[128,512]{1,0:T(32,128)(4,1)S(1)}, ...), condition=%wide.region_2.2_spmd, body=%wide.region_1.1_spmd.sunk | while | flops 17313792 | bytes 1065029 | solution.py:45
  112.3 4.9 %collective-permute-done = f32[512,32]{0,1:T(8,128)S(1)} collective-permute-done((f32[512,32]{0,1:T(8,128)S(1)}, f32[512,32]{0,1:T(8,128)S(1)}, u32[]{:S(2)}, u32[]{:S(2)}) %collective-permute-start) | collective-permute-done | bytes 65568 | tf_op jit(solution)/shard_map/while/body/eval_jaxpr/ppermute | solution.py:46
  117.1 1.0 constant_dynamic-slice_fusion.4
  118.1 2.9 %while.54 = (s32[]{:T(128)}, f32[128,32]{0,1:T(8,128)S(1)}, f32[512,32]{0,1:T(8,128)S(1)}, f32[128,512]{1,0:T(8,128)S(1)}, pred[128,512]{1,0:T(32,128)(4,1)S(1)}, /*index=5*/s32[]{:T(128)}) while((s32[]{:T(128)}, f32[128,32]{0,1:T(8,128)S(1)}, f32[512,32]{0,1:T(8,128)S(1)}, f32[128,512]{1,0:T(8,128)S(1)}, pred[128,512]{1,0:T(32,128)(4,1)S(1)}, ...), condition=%wide.region_2.2_spmd, body=%wide.region_1.1_spmd.sunk | while | flops 17313792 | bytes 1065029 | solution.py:45
  121.1 4.9 %collective-permute-done = f32[512,32]{0,1:T(8,128)S(1)} collective-permute-done((f32[512,32]{0,1:T(8,128)S(1)}, f32[512,32]{0,1:T(8,128)S(1)}, u32[]{:S(2)}, u32[]{:S(2)}) %collective-permute-start) | collective-permute-done | bytes 65568 | tf_op jit(solution)/shard_map/while/body/eval_jaxpr/ppermute | solution.py:46
  126.9 2.9 %while.54 = (s32[]{:T(128)}, f32[128,32]{0,1:T(8,128)S(1)}, f32[512,32]{0,1:T(8,128)S(1)}, f32[128,512]{1,0:T(8,128)S(1)}, pred[128,512]{1,0:T(32,128)(4,1)S(1)}, /*index=5*/s32[]{:T(128)}) while((s32[]{:T(128)}, f32[128,32]{0,1:T(8,128)S(1)}, f32[512,32]{0,1:T(8,128)S(1)}, f32[128,512]{1,0:T(8,128)S(1)}, pred[128,512]{1,0:T(32,128)(4,1)S(1)}, ...), condition=%wide.region_2.2_spmd, body=%wide.region_1.1_spmd.sunk | while | flops 17313792 | bytes 1065029 | solution.py:45
  129.9 4.9 %collective-permute-done = f32[512,32]{0,1:T(8,128)S(1)} collective-permute-done((f32[512,32]{0,1:T(8,128)S(1)}, f32[512,32]{0,1:T(8,128)S(1)}, u32[]{:S(2)}, u32[]{:S(2)}) %collective-permute-start) | collective-permute-done | bytes 65568 | tf_op jit(solution)/shard_map/while/body/eval_jaxpr/ppermute | solution.py:46
  135.7 2.9 %while.54 = (s32[]{:T(128)}, f32[128,32]{0,1:T(8,128)S(1)}, f32[512,32]{0,1:T(8,128)S(1)}, f32[128,512]{1,0:T(8,128)S(1)}, pred[128,512]{1,0:T(32,128)(4,1)S(1)}, /*index=5*/s32[]{:T(128)}) while((s32[]{:T(128)}, f32[128,32]{0,1:T(8,128)S(1)}, f32[512,32]{0,1:T(8,128)S(1)}, f32[128,512]{1,0:T(8,128)S(1)}, pred[128,512]{1,0:T(32,128)(4,1)S(1)}, ...), condition=%wide.region_2.2_spmd, body=%wide.region_1.1_spmd.sunk | while | flops 17313792 | bytes 1065029 | solution.py:45
  138.7 4.9 %collective-permute-done = f32[512,32]{0,1:T(8,128)S(1)} collective-permute-done((f32[512,32]{0,1:T(8,128)S(1)}, f32[512,32]{0,1:T(8,128)S(1)}, u32[]{:S(2)}, u32[]{:S(2)}) %collective-permute-start) | collective-permute-done | bytes 65568 | tf_op jit(solution)/shard_map/while/body/eval_jaxpr/ppermute | solution.py:46
  (314 shorter events, 47.7 us)
Async XLA Ops:
  0.6 1.9 %copy-start.3 = (f32[128,32]{0,1:T(8,128)S(1)}, f32[128,32]{0,1:T(8,128)}, u32[]{:S(2)}) copy-start(f32[128,32]{0,1:T(8,128)} %param.10) | copy-start | bytes 49156
  0.6 1.9 %copy-start.1 = (f32[512,32]{0,1:T(8,128)S(1)}, f32[512,32]{0,1:T(8,128)}, u32[]{:S(2)}) copy-start(f32[512,32]{0,1:T(8,128)} %param.11) | copy-start | bytes 196612
  6.5 4.9 %collective-permute-start = (f32[512,32]{0,1:T(8,128)S(1)}, f32[512,32]{0,1:T(8,128)S(1)}, u32[]{:S(2)}, u32[]{:S(2)}) collective-permute-start(f32[512,32]{0,1:T(8,128)S(1)} %get-tuple-element.291), channel_id=1, source_target_pairs={{0,7},{1,0},{2,1},{3,2},{4,3},{5,4},{6,5},{7,6},{8,15},{9,8},{10,9... | collective-permute-start | bytes 196616 | tf_op jit(solution)/shard_map/while/body/eval_jaxpr/ppermute | solution.py:46
  15.3 4.9 %collective-permute-start = (f32[512,32]{0,1:T(8,128)S(1)}, f32[512,32]{0,1:T(8,128)S(1)}, u32[]{:S(2)}, u32[]{:S(2)}) collective-permute-start(f32[512,32]{0,1:T(8,128)S(1)} %get-tuple-element.291), channel_id=1, source_target_pairs={{0,7},{1,0},{2,1},{3,2},{4,3},{5,4},{6,5},{7,6},{8,15},{9,8},{10,9... | collective-permute-start | bytes 196616 | tf_op jit(solution)/shard_map/while/body/eval_jaxpr/ppermute | solution.py:46
  24.1 4.9 %collective-permute-start = (f32[512,32]{0,1:T(8,128)S(1)}, f32[512,32]{0,1:T(8,128)S(1)}, u32[]{:S(2)}, u32[]{:S(2)}) collective-permute-start(f32[512,32]{0,1:T(8,128)S(1)} %get-tuple-element.291), channel_id=1, source_target_pairs={{0,7},{1,0},{2,1},{3,2},{4,3},{5,4},{6,5},{7,6},{8,15},{9,8},{10,9... | collective-permute-start | bytes 196616 | tf_op jit(solution)/shard_map/while/body/eval_jaxpr/ppermute | solution.py:46
  32.9 4.9 %collective-permute-start = (f32[512,32]{0,1:T(8,128)S(1)}, f32[512,32]{0,1:T(8,128)S(1)}, u32[]{:S(2)}, u32[]{:S(2)}) collective-permute-start(f32[512,32]{0,1:T(8,128)S(1)} %get-tuple-element.291), channel_id=1, source_target_pairs={{0,7},{1,0},{2,1},{3,2},{4,3},{5,4},{6,5},{7,6},{8,15},{9,8},{10,9... | collective-permute-start | bytes 196616 | tf_op jit(solution)/shard_map/while/body/eval_jaxpr/ppermute | solution.py:46
  41.7 4.9 %collective-permute-start = (f32[512,32]{0,1:T(8,128)S(1)}, f32[512,32]{0,1:T(8,128)S(1)}, u32[]{:S(2)}, u32[]{:S(2)}) collective-permute-start(f32[512,32]{0,1:T(8,128)S(1)} %get-tuple-element.291), channel_id=1, source_target_pairs={{0,7},{1,0},{2,1},{3,2},{4,3},{5,4},{6,5},{7,6},{8,15},{9,8},{10,9... | collective-permute-start | bytes 196616 | tf_op jit(solution)/shard_map/while/body/eval_jaxpr/ppermute | solution.py:46
  50.5 4.9 %collective-permute-start = (f32[512,32]{0,1:T(8,128)S(1)}, f32[512,32]{0,1:T(8,128)S(1)}, u32[]{:S(2)}, u32[]{:S(2)}) collective-permute-start(f32[512,32]{0,1:T(8,128)S(1)} %get-tuple-element.291), channel_id=1, source_target_pairs={{0,7},{1,0},{2,1},{3,2},{4,3},{5,4},{6,5},{7,6},{8,15},{9,8},{10,9... | collective-permute-start | bytes 196616 | tf_op jit(solution)/shard_map/while/body/eval_jaxpr/ppermute | solution.py:46
  59.3 4.9 %collective-permute-start = (f32[512,32]{0,1:T(8,128)S(1)}, f32[512,32]{0,1:T(8,128)S(1)}, u32[]{:S(2)}, u32[]{:S(2)}) collective-permute-start(f32[512,32]{0,1:T(8,128)S(1)} %get-tuple-element.291), channel_id=1, source_target_pairs={{0,7},{1,0},{2,1},{3,2},{4,3},{5,4},{6,5},{7,6},{8,15},{9,8},{10,9... | collective-permute-start | bytes 196616 | tf_op jit(solution)/shard_map/while/body/eval_jaxpr/ppermute | solution.py:46
  68.1 4.9 %collective-permute-start = (f32[512,32]{0,1:T(8,128)S(1)}, f32[512,32]{0,1:T(8,128)S(1)}, u32[]{:S(2)}, u32[]{:S(2)}) collective-permute-start(f32[512,32]{0,1:T(8,128)S(1)} %get-tuple-element.291), channel_id=1, source_target_pairs={{0,7},{1,0},{2,1},{3,2},{4,3},{5,4},{6,5},{7,6},{8,15},{9,8},{10,9... | collective-permute-start | bytes 196616 | tf_op jit(solution)/shard_map/while/body/eval_jaxpr/ppermute | solution.py:46
  76.9 4.9 %collective-permute-start = (f32[512,32]{0,1:T(8,128)S(1)}, f32[512,32]{0,1:T(8,128)S(1)}, u32[]{:S(2)}, u32[]{:S(2)}) collective-permute-start(f32[512,32]{0,1:T(8,128)S(1)} %get-tuple-element.291), channel_id=1, source_target_pairs={{0,7},{1,0},{2,1},{3,2},{4,3},{5,4},{6,5},{7,6},{8,15},{9,8},{10,9... | collective-permute-start | bytes 196616 | tf_op jit(solution)/shard_map/while/body/eval_jaxpr/ppermute | solution.py:46
  85.8 4.9 %collective-permute-start = (f32[512,32]{0,1:T(8,128)S(1)}, f32[512,32]{0,1:T(8,128)S(1)}, u32[]{:S(2)}, u32[]{:S(2)}) collective-permute-start(f32[512,32]{0,1:T(8,128)S(1)} %get-tuple-element.291), channel_id=1, source_target_pairs={{0,7},{1,0},{2,1},{3,2},{4,3},{5,4},{6,5},{7,6},{8,15},{9,8},{10,9... | collective-permute-start | bytes 196616 | tf_op jit(solution)/shard_map/while/body/eval_jaxpr/ppermute | solution.py:46
  94.6 4.9 %collective-permute-start = (f32[512,32]{0,1:T(8,128)S(1)}, f32[512,32]{0,1:T(8,128)S(1)}, u32[]{:S(2)}, u32[]{:S(2)}) collective-permute-start(f32[512,32]{0,1:T(8,128)S(1)} %get-tuple-element.291), channel_id=1, source_target_pairs={{0,7},{1,0},{2,1},{3,2},{4,3},{5,4},{6,5},{7,6},{8,15},{9,8},{10,9... | collective-permute-start | bytes 196616 | tf_op jit(solution)/shard_map/while/body/eval_jaxpr/ppermute | solution.py:46
  103.4 4.9 %collective-permute-start = (f32[512,32]{0,1:T(8,128)S(1)}, f32[512,32]{0,1:T(8,128)S(1)}, u32[]{:S(2)}, u32[]{:S(2)}) collective-permute-start(f32[512,32]{0,1:T(8,128)S(1)} %get-tuple-element.291), channel_id=1, source_target_pairs={{0,7},{1,0},{2,1},{3,2},{4,3},{5,4},{6,5},{7,6},{8,15},{9,8},{10,9... | collective-permute-start | bytes 196616 | tf_op jit(solution)/shard_map/while/body/eval_jaxpr/ppermute | solution.py:46
  112.2 4.9 %collective-permute-start = (f32[512,32]{0,1:T(8,128)S(1)}, f32[512,32]{0,1:T(8,128)S(1)}, u32[]{:S(2)}, u32[]{:S(2)}) collective-permute-start(f32[512,32]{0,1:T(8,128)S(1)} %get-tuple-element.291), channel_id=1, source_target_pairs={{0,7},{1,0},{2,1},{3,2},{4,3},{5,4},{6,5},{7,6},{8,15},{9,8},{10,9... | collective-permute-start | bytes 196616 | tf_op jit(solution)/shard_map/while/body/eval_jaxpr/ppermute | solution.py:46
  121.0 4.9 %collective-permute-start = (f32[512,32]{0,1:T(8,128)S(1)}, f32[512,32]{0,1:T(8,128)S(1)}, u32[]{:S(2)}, u32[]{:S(2)}) collective-permute-start(f32[512,32]{0,1:T(8,128)S(1)} %get-tuple-element.291), channel_id=1, source_target_pairs={{0,7},{1,0},{2,1},{3,2},{4,3},{5,4},{6,5},{7,6},{8,15},{9,8},{10,9... | collective-permute-start | bytes 196616 | tf_op jit(solution)/shard_map/while/body/eval_jaxpr/ppermute | solution.py:46
  129.8 4.9 %collective-permute-start = (f32[512,32]{0,1:T(8,128)S(1)}, f32[512,32]{0,1:T(8,128)S(1)}, u32[]{:S(2)}, u32[]{:S(2)}) collective-permute-start(f32[512,32]{0,1:T(8,128)S(1)} %get-tuple-element.291), channel_id=1, source_target_pairs={{0,7},{1,0},{2,1},{3,2},{4,3},{5,4},{6,5},{7,6},{8,15},{9,8},{10,9... | collective-permute-start | bytes 196616 | tf_op jit(solution)/shard_map/while/body/eval_jaxpr/ppermute | solution.py:46
  138.6 4.9 %collective-permute-start = (f32[512,32]{0,1:T(8,128)S(1)}, f32[512,32]{0,1:T(8,128)S(1)}, u32[]{:S(2)}, u32[]{:S(2)}) collective-permute-start(f32[512,32]{0,1:T(8,128)S(1)} %get-tuple-element.291), channel_id=1, source_target_pairs={{0,7},{1,0},{2,1},{3,2},{4,3},{5,4},{6,5},{7,6},{8,15},{9,8},{10,9... | collective-permute-start | bytes 196616 | tf_op jit(solution)/shard_map/while/body/eval_jaxpr/ppermute | solution.py:46
  143.6 0.6 copy-start
  143.6 0.6 copy-start.2
where the time goes:
time: 145 us; the launch traced here: 144 us
  waiting for transfers between devices  77.4 us (53%)
  matrix products  42.6 us (29%)
  local copies, waits for them, and re-layouts  17.1 us (12%)
  loops' own time  2.82 us (2%)
  other arithmetic  1.9 us (1%)
  starting transfers between devices  1.62 us (1%)
    ppermute x16, waiting for transfers between devices, stratum(): item_blk = lax.ppermute(item_blk, 'shard', shift_back)  77.4 us
    dot_general x64, matrix products, step(): jnp.einsum('ui,ur->ir', residual, user_bf, preferred_element_type=jnp.flo...  21.5 us
    dot_general x64, matrix products, step(): grad_user = jnp.dot(residual, item_bf, preferred_element_type=jnp.float32)  21.2 us
    dynamic_slice x16, local copies, waits for them, and re-layouts, stratum(): rating_blk = lax.dynamic_slice_in_dim(ratings, col_start, items_dev, axis=1)  15.6 us
  transfers between devices with their start and end apart: 16, of which 16 were waited for; matrix products, arithmetic and copies ran while one was open for 0% of the time, Pallas kernels for 0%

commit v1 on v0

v1 whole, which is shorter than its diff:
```python
import functools
import math

import jax
import jax.numpy as jnp
from jax import lax
from jax.experimental import pallas as pl
from jax.experimental.pallas import tpu as pltpu
from jax.sharding import PartitionSpec as P

STRATUM_STEPS = 4
EPOCHS = 2
MESH = pl.DeviceIdType.MESH
BF16 = jnp.bfloat16
F32 = jnp.float32


def kernel(group, ratings, observed, user_t, item_t, user_out, item_out,
           rate, seen, held, sent, rate_sem, seen_sem, send_sem, recv_sem):
    me = lax.axis_index("shard")
    left, right = lax.rem(me + group - 1, group), lax.rem(me + 1, group)
    rank, users = user_t.shape
    items = item_t.shape[1]
    step_scale = (users + items + rank) / math.sqrt(rank)
    step_size = 0.5 / step_scale
    weight_decay = 0.03 * math.sqrt(users * items / rank)
    strata = EPOCHS * group

    def fetches(stratum):
        start = pl.multiple_of(lax.rem(me + stratum, group) * items, items)
        return (
            pltpu.make_async_copy(ratings.at[:, pl.ds(start, items)], rate.at[stratum], rate_sem.at[stratum]),
            pltpu.make_async_copy(observed.at[:, pl.ds(start, items)], seen.at[stratum], seen_sem.at[stratum]),
        )

    for stratum in range(group):
        for fetch in fetches(stratum):
            fetch.start()

    barrier = pltpu.get_barrier_semaphore()
    for neighbour in (left, right):
        pl.semaphore_signal(barrier, inc=1, device_id={"shard": neighbour}, device_id_type=MESH)
    pl.semaphore_wait(barrier, 2)

    held[0] = item_t[...]

    def hop(stratum):
        return pltpu.make_async_remote_copy(
            src_ref=sent.at[stratum],
            dst_ref=held.at[stratum + 1],
            send_sem=send_sem.at[stratum],
            recv_sem=recv_sem.at[stratum],
            device_id={"shard": left},
            device_id_type=MESH,
        )

    def half(user_bf, item_bf, seen_blk, rate_blk):
        predicted = jnp.dot(user_bf, item_bf, preferred_element_type=F32)
        return jnp.where(seen_blk, predicted - rate_blk, 0.0).astype(BF16)

    def stratum_body(stratum, user):
        block = lax.rem(stratum, group)

        @pl.when(stratum < group)
        def _():
            for fetch in fetches(block):
                fetch.wait()

        @pl.when(stratum > 0)
        def _():
            hop(stratum - 1).wait_recv()

        item = held[stratum]
        for _ in range(STRATUM_STEPS):
            item_bf = item.astype(BF16)
            residual = half(user.astype(BF16), item_bf, seen[block] != 0, rate[block])
            grad_user = lax.dot_general(residual, item_bf, (((1,), (1,)), ((), ())), preferred_element_type=F32)
            user = user - step_size * (grad_user + weight_decay * user)
            user_bf = user.astype(BF16)
            residual = half(user_bf, item_bf, seen[block] != 0, rate[block])
            grad_item = jnp.dot(user_bf.T, residual, preferred_element_type=F32)
            item = item - step_size * (grad_item + weight_decay * item)
        sent[stratum] = item
        hop(stratum).start()
        return user

    user = lax.fori_loop(0, strata, stratum_body, user_t[...].T)
    user_out[...] = user.T
    for stratum in range(strata):
        hop(stratum).wait_send()
    hop(strata - 1).wait_recv()
    item_out[...] = held[strata]


def solution(mesh):
    group = mesh.shape["shard"]
    row_spec = P(("rep", "shard"), None)
    strata = EPOCHS * group

    def local(ratings, observed, user_init, item_init):
        users, rank = user_init.shape
        items = item_init.shape[0]
        vmem = pl.BlockSpec(memory_space=pltpu.VMEM)
        hbm = pl.BlockSpec(memory_space=pl.ANY)
        user_t, item_t = pl.pallas_call(
            functools.partial(kernel, group),
            out_shape=(
                jax.ShapeDtypeStruct((rank, users), F32),
                jax.ShapeDtypeStruct((rank, items), F32),
            ),
            in_specs=[hbm, hbm, vmem, vmem],
            out_specs=(vmem, vmem),
            scratch_shapes=[
                pltpu.VMEM((group, users, items), F32),
                pltpu.VMEM((group, users, items), jnp.int32),
                pltpu.VMEM((strata + 1, rank, items), F32),
                pltpu.VMEM((strata, rank, items), F32),
                pltpu.SemaphoreType.DMA((group,)),
                pltpu.SemaphoreType.DMA((group,)),
                pltpu.SemaphoreType.DMA((strata,)),
                pltpu.SemaphoreType.DMA((strata,)),
            ],
            compiler_params=pltpu.CompilerParams(collective_id=0, has_side_effects=True),
        )(ratings, observed, user_init.T, item_init.T)
        return user_t.T, item_t.T

    return jax.shard_map(local, mesh=mesh, in_specs=(row_spec,) * 4, out_specs=(row_spec, row_spec), check_vma=False)
```

time: 145 us -> 77.3 us (0.53)
  the two profiles are of different devices: /device:TPU:95 before, /device:TPU:81 now
where the time goes in v1:
time: 77.3 us; the launch traced here: 77 us
  Pallas kernels  73.6 us (95%)
  local copies, waits for them, and re-layouts  2.8 us (4%)
    pallas_call x1, Pallas kernels, local(): pl.pallas_call(functools.partial(kernel, group), out_shape=(jax.ShapeDtyp...  73.6 us
    unnamed x2, local copies, waits for them, and re-layouts  2.8 us

profile of v1, /device:TPU:81, one launch (start us, length us, event | category | flops | bytes accessed | tf_op | source)
XLA Modules:
  0.0 77.0 jit_solution(16241339977749807006)
XLA Ops:
  0.6 73.6 %shard_map.59 = (f32[32,128]{1,0:T(8,128)}, f32[32,512]{1,0:T(8,128)}) custom-call(f32[128,4096]{1,0:T(8,128)} %ratings.1, s32[128,4096]{1,0:T(8,128)} %observed.1, f32[32,128]{1,0:T(8,128)} %bitcast.6, f32[32,512]{1,0:T(8,128)} %bitcast.4), custom_call_target="tpu_custom_call" | custom-call | tf_op jit(solution)/shard_map/pallas_call | solution.py:105
  74.2 1.3 %copy.8 = f32[128,32]{0,1:T(8,128)} copy(f32[128,32]{0,1:T(8,128)} %bitcast.7) | data formatting | bytes 32768
  75.5 1.5 %copy.9 = f32[512,32]{0,1:T(8,128)} copy(f32[512,32]{0,1:T(8,128)} %bitcast.5) | data formatting | bytes 131072
